TPU v7x, 256 devices: a whole 4x4x8 slice. The times are simulated.
256 devices in a mesh: dp: 8 (over z), vocab: 32 (over x, y, core).
Axes of the slice: x: 4, y: 4, z: 8, core: 2. Of those that a mesh axis runs over, the one named last changes fastest.
Arguments:
- token_ids: int32 [65536], P(('dp', 'vocab')), may hold values from 0 to 152063, as said below
- token_count: int32 [256], P(('dp', 'vocab')), may hold values from 16 to 256
- out_grads: bfloat16 [65536, 5120], P(('dp', 'vocab')), may hold values from -18 to 18
- master_rows: float32 [16384, 5120], P('vocab', 'dp'), may hold values from -0.8 to 0.8
- first_moment: float32 [16384, 5120], P('vocab', 'dp'), may hold values from -4 to 4
- second_moment: float32 [16384, 5120], P('vocab', 'dp'), may hold values from 0.001 to 1
Outputs:
- new_master: float32 [16384, 5120], P('vocab', 'dp')
- new_first: float32 [16384, 5120], P('vocab', 'dp')
- new_second: float32 [16384, 5120], P('vocab', 'dp')
- table_rows: bfloat16 [16384, 5120], P('vocab')
Inputs may be any that keep to these rules, and one draw needn't show every extreme that they name: `token_ids`: within each block of 256 slots, among the live slots (the first token_count of the block) at most 8 have ids in the new rows j * 512 + 135680 to (j + 1) * 512 + 135679 for any one j, and for some j exactly 8 in every block. Slots past token_count hold ids of new rows that are to be ignored.
All inputs are finite; a program needn't handle non-finite values.
Results may differ from a plain program's by a relative error of at most 0.001.
Values may be sent and summed in bfloat16 or wider, within the bound.
No kernel may reach another device: no remote copies, remote signals or barrier semaphores. Data moves between devices by JAX's collectives and lax.ppermute only.
A program may use at most 64 MiB of HBM per device.

v0:
```python
import jax
import jax.numpy as jnp
from jax import lax
from jax.sharding import PartitionSpec as P

VOCAB = 152064
CAP = 8
beta_one = 0.9
beta_two = 0.999
corr_one = 1.0 - 0.9**10
corr_two = 1.0 - 0.999**10
learn_rate = 0.01
epsilon = 1e-08


def body(token_ids, token_count, out_grads, master_rows, first_moment, second_moment):
    owners = lax.axis_size("vocab")
    groups = lax.axis_size("dp")
    rows_own = master_rows.shape[0]
    tok_slots = token_ids.shape[0]
    first_new = VOCAB - rows_own * owners
    position = jnp.arange(tok_slots)
    is_live = (position < token_count[0]) & (token_ids >= first_new)
    new_index = token_ids - first_new
    owner_of = new_index // rows_own
    row_in_owner = new_index % rows_own
    belongs = (owner_of[:, None] == jnp.arange(owners)[None, :]) & is_live[:, None]
    ranking = jnp.cumsum(belongs.astype(jnp.int32), axis=0) - 1
    my_rank = jnp.sum(jnp.where(belongs, ranking, 0), axis=1)
    slot_index = jnp.where(is_live, owner_of * CAP + my_rank, -1)
    placing = jnp.arange(owners * CAP)[:, None] == slot_index[None, :]
    outgoing = jnp.dot(
        placing.astype(jnp.bfloat16), out_grads, preferred_element_type=jnp.float32
    ).astype(jnp.bfloat16)
    slot_row = jnp.max(jnp.where(placing, row_in_owner[None, :], -1), axis=1)
    upper_part = jnp.where(slot_row >= 0, slot_row // 16, -1)
    lower_part = jnp.where(slot_row >= 0, slot_row % 16, 0)
    row_pairs = jnp.stack([upper_part, lower_part], axis=1).astype(jnp.bfloat16)
    tiled_pairs = jnp.tile(row_pairs, (1, groups))
    split_grads, split_pairs = (
        lax.all_to_all(outgoing, "dp", split_axis=1, concat_axis=0, tiled=True),
        lax.all_to_all(tiled_pairs, "dp", split_axis=1, concat_axis=0, tiled=True),
    )
    split_grads = split_grads.reshape(groups, owners * CAP, split_grads.shape[1])
    split_pairs = split_pairs.reshape(groups, owners * CAP, 2)
    arrived, arrived_pairs = (
        lax.all_to_all(split_grads, "vocab", split_axis=1, concat_axis=0, tiled=True),
        lax.all_to_all(split_pairs, "vocab", split_axis=1, concat_axis=0, tiled=True),
    )
    arrived = arrived.reshape(-1, arrived.shape[2])
    arrived_pairs = arrived_pairs.reshape(-1, 2).astype(jnp.float32)
    decoded = arrived_pairs[:, 0] * 16.0 + arrived_pairs[:, 1]
    selector = decoded[None, :] == jnp.arange(rows_own, dtype=jnp.float32)[:, None]
    gradient = jnp.dot(selector.astype(jnp.bfloat16), arrived, preferred_element_type=jnp.float32)
    new_first = beta_one * first_moment + (1.0 - beta_one) * gradient
    new_second = beta_two * second_moment + (1.0 - beta_two) * gradient * gradient
    update = new_first / corr_one / (jnp.sqrt(new_second / corr_two) + epsilon)
    new_master = master_rows - learn_rate * update
    table_rows = lax.all_gather(new_master.astype(jnp.bfloat16), "dp", axis=1, tiled=True)
    return (new_master, new_first, new_second, table_rows)


def solution(mesh):
    return jax.shard_map(
        body,
        mesh=mesh,
        in_specs=(
            P(("dp", "vocab")),
            P(("dp", "vocab")),
            P(("dp", "vocab"), None),
            P("vocab", "dp"),
            P("vocab", "dp"),
            P("vocab", "dp"),
        ),
        out_specs=(P("vocab", "dp"), P("vocab", "dp"), P("vocab", "dp"), P("vocab", None)),
        check_vma=False,
    )
```

profile of v0, /device:TPU:1, one launch (start us, length us, event | category | flops | bytes accessed | tf_op | source)
XLA Modules:
  0.0 226.1 jit_solution(13173120727746846813)
XLA Ops:
  7.2 0.0 copy-start
  8.0 0.7 and_select_fusion.2
  8.7 0.7 fusion.15
  9.4 0.7 compare_and_fusion
  10.0 0.6 reduce-window.6
  10.6 0.2 slice_reduce_fusion
  10.9 0.1 fusion.5
  11.0 0.7 add_select_fusion
  11.7 0.1 select_reduce_fusion
  11.8 0.6 tile.2
  12.4 9.0 %all-to-all-start = ((bf16[256,8,2]{0,2,1:T(2,128)(2,1)}), bf16[256,8,2]{0,2,1:T(2,128)(2,1)S(1)}, u32[]{:S(2)}, u32[]{:S(2)}) async-start(bf16[256,8,2]{0,2,1:T(2,128)(2,1)} %tile.2), calls=%async_computation | async-start | bytes 16384 | tf_op jit(solution)/shard_map/all_to_all | solution.py:42
  21.4 0.0 copy-done
  21.4 0.8 convolution_convert_fusion
  22.3 1.7 copy.51
  24.0 4.0 %all-to-all-done = bf16[256,8,2]{0,2,1:T(2,128)(2,1)S(1)} async-done(((bf16[256,8,2]{0,2,1:T(2,128)(2,1)}), bf16[256,8,2]{0,2,1:T(2,128)(2,1)S(1)}, u32[]{:S(2)}, u32[]{:S(2)}) %all-to-all-start) | async-done | bytes 8224 | tf_op jit(solution)/shard_map/all_to_all | solution.py:42
  28.0 4.4 %all-to-all-start.2 = ((bf16[256,8,640]{2,0,1:T(8,128)(2,1)}), bf16[256,8,640]{2,0,1:T(8,128)(2,1)}, u32[]{:S(2)}, u32[]{:S(2)}) async-start(bf16[256,8,640]{2,0,1:T(8,128)(2,1)} %bitcast.43), calls=%async_computation.2 | async-start | bytes 5242880 | tf_op jit(solution)/shard_map/all_to_all | solution.py:41
  32.4 0.8 copy.39
  33.2 58.8 %all-to-all-done.2 = bf16[256,8,640]{2,0,1:T(8,128)(2,1)} async-done(((bf16[256,8,640]{2,0,1:T(8,128)(2,1)}), bf16[256,8,640]{2,0,1:T(8,128)(2,1)}, u32[]{:S(2)}, u32[]{:S(2)}) %all-to-all-start.2) | async-done | bytes 2621472 | tf_op jit(solution)/shard_map/all_to_all | solution.py:41
  92.0 10.9 %all-to-all-start.1 = ((bf16[8,256,2]{0,2,1:T(2,128)(2,1)}), bf16[8,256,2]{0,2,1:T(2,128)(2,1)S(1)}, u32[]{:S(2)}, u32[]{:S(2)}) async-start(bf16[8,256,2]{0,2,1:T(2,128)(2,1)} %copy.39), calls=%async_computation.1 | async-start | bytes 262144 | tf_op jit(solution)/shard_map/all_to_all | solution.py:48
  103.0 4.7 %copy.43 = bf16[8,256,640]{2,0,1:T(8,128)(2,1)} copy(bf16[8,256,640]{2,1,0:T(8,128)(2,1)} %bitcast.8) | data formatting | bytes 5242880 | tf_op jit(solution)/shard_map/all_to_all | solution.py:41
  107.7 2.9 %all-to-all-done.1 = bf16[8,256,2]{0,2,1:T(2,128)(2,1)S(1)} async-done(((bf16[8,256,2]{0,2,1:T(2,128)(2,1)}), bf16[8,256,2]{0,2,1:T(2,128)(2,1)S(1)}, u32[]{:S(2)}, u32[]{:S(2)}) %all-to-all-start.1) | async-done | bytes 8224 | tf_op jit(solution)/shard_map/all_to_all | solution.py:48
  110.7 4.8 %all-to-all-start.3 = ((bf16[8,256,640]{2,0,1:T(8,128)(2,1)}), bf16[8,256,640]{2,0,1:T(8,128)(2,1)}, u32[]{:S(2)}, u32[]{:S(2)}) async-start(bf16[8,256,640]{2,0,1:T(8,128)(2,1)} %copy.43), calls=%async_computation.3 | async-start | bytes 5242880 | tf_op jit(solution)/shard_map/all_to_all | solution.py:47
  115.4 0.0 all-gather.2.cloned.1.call-start
  115.5 0.1 copy.40
  115.6 0.2 reshape.169
  115.8 0.2 copy.41
  115.9 0.2 reshape.168
  116.1 33.4 %all-to-all-done.3 = bf16[8,256,640]{2,0,1:T(8,128)(2,1)} async-done(((bf16[8,256,640]{2,0,1:T(8,128)(2,1)}), bf16[8,256,640]{2,0,1:T(8,128)(2,1)}, u32[]{:S(2)}, u32[]{:S(2)}) %all-to-all-start.3) | async-done | bytes 2621472 | tf_op jit(solution)/shard_map/all_to_all | solution.py:47
  149.5 0.0 copy-start.1
  149.5 0.0 copy-start.2
  149.5 0.0 copy-start.3
  149.5 2.4 %copy.45 = bf16[32,8,8,640]{3,2,1,0:T(8,128)(2,1)S(1)} copy(bf16[32,8,8,640]{3,1,2,0:T(8,128)(2,1)} %bitcast.11) | data formatting | bytes 5242880 | tf_op jit(solution)/shard_map/all_to_all | solution.py:47
  151.9 0.0 copy-done.1
  151.9 0.1 copy-done.2
  152.0 0.4 copy-done.3
  152.4 4.7 %fusion.11 = (bf16[512,640]{1,0:T(8,128)(2,1)}, f32[512,640]{1,0:T(8,128)}, f32[512,640]{1,0:T(8,128)}, f32[512,640]{1,0:T(8,128)}) fusion(f32[512,640]{1,0:T(8,128)S(1)} %copy-done.1, f32[512,640]{1,0:T(8,128)S(1)} %copy-done.2, f32[512,640]{1,0:T(8,128)S(1)} %copy-done.3, bf16[2048,640]{1,0:T(8,128)(2,1)S(1)} %bitcast.45, f32[2048]{0:T(1024)S(1)} %bitcast.49), kind=kOutput, calls=%fused_computation.43 | convolution fusion | flops 1347813376 | bytes 11149312 | tf_op jit(solution)/shard_map/dot_general | solution.py:54
  157.1 0.0 all-gather.2.cloned.1.call-update
  157.1 57.0 %all-gather.2.cloned.1.call-done = bf16[512,5120]{1,0:T(8,128)(2,1)} async-done(((bf16[512,640]{1,0:T(8,128)(2,1)}), bf16[512,5120]{1,0:T(8,128)(2,1)}) %all-gather.2.cloned.1.call-update) | async-done | bytes 5242896 | tf_op jit(solution)/shard_map/all_gather | solution.py:59
  214.1 5.2 %copy.54 = bf16[512,5120]{1,0:T(8,128)(2,1)} copy(bf16[512,5120]{1,0:T(8,128)(2,1)} %all-gather.2.cloned.1.call-done) | data formatting | bytes 10485760
  (6 shorter events, 0.1 us)
Async XLA Ops:
  7.2 14.3 %copy-start = (bf16[256,5120]{1,0:T(8,128)(2,1)S(1)}, bf16[256,5120]{1,0:T(8,128)(2,1)}, u32[]{:S(2)}) copy-start(bf16[256,5120]{1,0:T(8,128)(2,1)} %param.8) | copy-start | bytes 7864324
  12.4 15.6 %all-to-all-start = ((bf16[256,8,2]{0,2,1:T(2,128)(2,1)}), bf16[256,8,2]{0,2,1:T(2,128)(2,1)S(1)}, u32[]{:S(2)}, u32[]{:S(2)}) async-start(bf16[256,8,2]{0,2,1:T(2,128)(2,1)} %tile.2), calls=%async_computation | async-start | bytes 16384 | tf_op jit(solution)/shard_map/all_to_all | solution.py:42
  28.0 64.0 %all-to-all-start.2 = ((bf16[256,8,640]{2,0,1:T(8,128)(2,1)}), bf16[256,8,640]{2,0,1:T(8,128)(2,1)}, u32[]{:S(2)}, u32[]{:S(2)}) async-start(bf16[256,8,640]{2,0,1:T(8,128)(2,1)} %bitcast.43), calls=%async_computation.2 | async-start | bytes 5242880 | tf_op jit(solution)/shard_map/all_to_all | solution.py:41
  92.0 18.6 %all-to-all-start.1 = ((bf16[8,256,2]{0,2,1:T(2,128)(2,1)}), bf16[8,256,2]{0,2,1:T(2,128)(2,1)S(1)}, u32[]{:S(2)}, u32[]{:S(2)}) async-start(bf16[8,256,2]{0,2,1:T(2,128)(2,1)} %copy.39), calls=%async_computation.1 | async-start | bytes 262144 | tf_op jit(solution)/shard_map/all_to_all | solution.py:48
  110.7 38.9 %all-to-all-start.3 = ((bf16[8,256,640]{2,0,1:T(8,128)(2,1)}), bf16[8,256,640]{2,0,1:T(8,128)(2,1)}, u32[]{:S(2)}, u32[]{:S(2)}) async-start(bf16[8,256,640]{2,0,1:T(8,128)(2,1)} %copy.43), calls=%async_computation.3 | async-start | bytes 5242880 | tf_op jit(solution)/shard_map/all_to_all | solution.py:47
  115.4 98.7 %all-gather.2.cloned.1.call-start = ((), (), s32[]{:S(2)}) async-start(), calls=%async_computation.4 | async-start | bytes 5898240 | tf_op jit(solution)/shard_map/all_gather | solution.py:59
  149.5 2.4 %copy-start.1 = (f32[512,640]{1,0:T(8,128)S(1)}, f32[512,640]{1,0:T(8,128)}, u32[]{:S(2)}) copy-start(f32[512,640]{1,0:T(8,128)} %param.9) | copy-start | bytes 3932164
  149.5 2.5 %copy-start.2 = (f32[512,640]{1,0:T(8,128)S(1)}, f32[512,640]{1,0:T(8,128)}, u32[]{:S(2)}) copy-start(f32[512,640]{1,0:T(8,128)} %param.10) | copy-start | bytes 3932164
  149.5 2.9 %copy-start.3 = (f32[512,640]{1,0:T(8,128)S(1)}, f32[512,640]{1,0:T(8,128)}, u32[]{:S(2)}) copy-start(f32[512,640]{1,0:T(8,128)} %param.11) | copy-start | bytes 3932164
Sparse Core Ops, SparseCore 0:
  157.2 56.8 all-gather.1
where the time goes:
time: 227 us; the launch traced here: 226 us
  waiting for transfers between devices  156 us (69%)
  starting transfers between devices  29.2 us (13%)
  local copies, waits for them, and re-layouts  16.7 us (7%)
  between operations  14.9 us (7%)
  matrix products  5.52 us (2%)
  other arithmetic  3.65 us (2%)
    all_to_all x1, waiting for transfers between devices, body(): lax.all_to_all(outgoing, 'dp', split_axis=1, concat_axis=0, tiled=True)  58.8 us
    all_gather x1, waiting for transfers between devices, body(): lax.all_gather(new_master.astype(jnp.bfloat16), 'dp', axis=1, tiled=True)  57 us
    all_to_all x1, waiting for transfers between devices, body(): lax.all_to_all(split_grads, 'vocab', split_axis=1, concat_axis=0, tiled=T...  33.4 us
    all_to_all x1, starting transfers between devices, body(): lax.all_to_all(split_pairs, 'vocab', split_axis=1, concat_axis=0, tiled=T...  10.9 us
    all_to_all x1, starting transfers between devices, body(): lax.all_to_all(tiled_pairs, 'dp', split_axis=1, concat_axis=0, tiled=True)  9 us
    all_to_all x2, local copies, waits for them, and re-layouts, body(): lax.all_to_all(outgoing, 'dp', split_axis=1, concat_axis=0, tiled=True)  6.47 us
    unnamed x9, local copies, waits for them, and re-layouts  5.69 us
    all_to_all x1, starting transfers between devices, body(): lax.all_to_all(split_grads, 'vocab', split_axis=1, concat_axis=0, tiled=T...  4.79 us
  transfers between devices with their start and end apart: 5, of which 5 were waited for; matrix products, arithmetic and copies ran while one was open for 4% of the time, Pallas kernels for 0%

commit v1 on v0

--- a/solution.py
+++ b/solution.py
@@ -11,6 +11,11 @@
 corr_two = 1.0 - 0.999**10
 learn_rate = 0.01
 epsilon = 1e-08
+
+
+def gather_over(x, axis, d):
+    stack = jnp.stack([x] * lax.axis_size(axis))
+    return jnp.concatenate(lax.all_to_all(stack, axis, 0, 0), axis=d)
 
 
 def body(token_ids, token_count, out_grads, master_rows, first_moment, second_moment):
@@ -56,7 +61,7 @@
     new_second = beta_two * second_moment + (1.0 - beta_two) * gradient * gradient
     update = new_first / corr_one / (jnp.sqrt(new_second / corr_two) + epsilon)
     new_master = master_rows - learn_rate * update
-    table_rows = lax.all_gather(new_master.astype(jnp.bfloat16), "dp", axis=1, tiled=True)
+    table_rows = gather_over(new_master.astype(jnp.bfloat16), "dp", 1)
     return (new_master, new_first, new_second, table_rows)
 
 

time: 227 us -> 288 us (1.27)
  blocking collectives: 0 us -> 121 us
  waiting for transfers between devices: 156 us -> 99.2 us
  between operations: 14.9 us -> 1.55 us
  local copies, waits for them, and re-layouts: 16.7 us -> 27.7 us
    all_to_all x0 -> x1, blocking collectives: none -> 121 us  [gather_over(): return jnp.concatenate(lax.all_to_all(stack, axis, 0, 0), axis=d)]
    all_gather x1 -> x0, waiting for transfers between devices: 57 us -> none  [body(): lax.all_gather(new_master.astype(jnp.bfloat16), 'dp', axis=1, tiled=True)]
    all_to_all x0 -> x1, local copies, waits for them, and re-layouts: none -> 7.87 us  [gather_over(): return jnp.concatenate(lax.all_to_all(stack, axis, 0, 0), axis=d)]
  transfers between devices with their start and end apart: 5 -> 4, of which waited for: 5 -> 4; matrix products, arithmetic and copies ran while one was open for 4% -> 3% of each run, Pallas kernels for 0% -> 0%
where the time goes in v1:
time: 288 us; the launch traced here: 287 us
  blocking collectives  121 us (42%)
  waiting for transfers between devices  99.2 us (34%)
  starting transfers between devices  29.1 us (10%)
  local copies, waits for them, and re-layouts  27.7 us (10%)
  matrix products  5.31 us (2%)
  other arithmetic  3.65 us (1%)
    all_to_all x1, blocking collectives, gather_over(): return jnp.concatenate(lax.all_to_all(stack, axis, 0, 0), axis=d)  121 us
    all_to_all x1, waiting for transfers between devices, body(): lax.all_to_all(outgoing, 'dp', split_axis=1, concat_axis=0, tiled=True)  58.8 us
    all_to_all x1, waiting for transfers between devices, body(): lax.all_to_all(split_grads, 'vocab', split_axis=1, concat_axis=0, tiled=T...  33.5 us
    all_to_all x1, starting transfers between devices, body(): lax.all_to_all(split_pairs, 'vocab', split_axis=1, concat_axis=0, tiled=T...  10.9 us
    all_to_all x1, starting transfers between devices, body(): lax.all_to_all(tiled_pairs, 'dp', split_axis=1, concat_axis=0, tiled=True)  9 us
    unnamed x9, local copies, waits for them, and re-layouts  8.42 us
    all_to_all x1, local copies, waits for them, and re-layouts, gather_over(): return jnp.concatenate(lax.all_to_all(stack, axis, 0, 0), axis=d)  7.87 us
    all_to_all x2, local copies, waits for them, and re-layouts, body(): lax.all_to_all(outgoing, 'dp', split_axis=1, concat_axis=0, tiled=True)  6.47 us
  transfers between devices with their start and end apart: 4, of which 4 were waited for; matrix products, arithmetic and copies ran while one was open for 3% of the time, Pallas kernels for 0%

profile of v1, /device:TPU:1, one launch (start us, length us, event | category | flops | bytes accessed | tf_op | source)
XLA Modules:
  0.0 287.1 jit_solution(15472980525736258792)
XLA Ops:
  0.6 0.0 copy-start
  1.4 0.7 and_select_fusion.2
  2.1 0.7 fusion.15
  2.8 0.7 compare_and_fusion
  3.5 0.6 reduce-window.6
  4.1 0.2 slice_reduce_fusion
  4.3 0.1 fusion.5
  4.4 0.7 add_select_fusion
  5.1 0.1 select_reduce_fusion
  5.3 0.6 tile.2
  5.9 9.0 %all-to-all-start = ((bf16[256,8,2]{0,2,1:T(2,128)(2,1)}), bf16[256,8,2]{0,2,1:T(2,128)(2,1)S(1)}, u32[]{:S(2)}, u32[]{:S(2)}) async-start(bf16[256,8,2]{0,2,1:T(2,128)(2,1)} %tile.2), calls=%async_computation | async-start | bytes 16384 | tf_op jit(solution)/shard_map/all_to_all | solution.py:47
  14.9 0.0 copy-done
  14.9 0.8 convolution_convert_fusion
  15.8 1.7 copy.65
  17.5 4.0 %all-to-all-done = bf16[256,8,2]{0,2,1:T(2,128)(2,1)S(1)} async-done(((bf16[256,8,2]{0,2,1:T(2,128)(2,1)}), bf16[256,8,2]{0,2,1:T(2,128)(2,1)S(1)}, u32[]{:S(2)}, u32[]{:S(2)}) %all-to-all-start) | async-done | bytes 8224 | tf_op jit(solution)/shard_map/all_to_all | solution.py:47
  21.5 4.4 %all-to-all-start.2 = ((bf16[256,8,640]{2,0,1:T(8,128)(2,1)}), bf16[256,8,640]{2,0,1:T(8,128)(2,1)}, u32[]{:S(2)}, u32[]{:S(2)}) async-start(bf16[256,8,640]{2,0,1:T(8,128)(2,1)} %bitcast.47), calls=%async_computation.2 | async-start | bytes 5242880 | tf_op jit(solution)/shard_map/all_to_all | solution.py:46
  25.9 0.8 copy.51
  26.7 58.8 %all-to-all-done.2 = bf16[256,8,640]{2,0,1:T(8,128)(2,1)} async-done(((bf16[256,8,640]{2,0,1:T(8,128)(2,1)}), bf16[256,8,640]{2,0,1:T(8,128)(2,1)}, u32[]{:S(2)}, u32[]{:S(2)}) %all-to-all-start.2) | async-done | bytes 2621472 | tf_op jit(solution)/shard_map/all_to_all | solution.py:46
  85.5 10.9 %all-to-all-start.1 = ((bf16[8,256,2]{0,2,1:T(2,128)(2,1)}), bf16[8,256,2]{0,2,1:T(2,128)(2,1)S(1)}, u32[]{:S(2)}, u32[]{:S(2)}) async-start(bf16[8,256,2]{0,2,1:T(2,128)(2,1)} %copy.51), calls=%async_computation.1 | async-start | bytes 262144 | tf_op jit(solution)/shard_map/all_to_all | solution.py:53
  96.4 4.7 %copy.55 = bf16[8,256,640]{2,0,1:T(8,128)(2,1)} copy(bf16[8,256,640]{2,1,0:T(8,128)(2,1)} %bitcast.8) | data formatting | bytes 5242880 | tf_op jit(solution)/shard_map/all_to_all | solution.py:46
  101.2 2.9 %all-to-all-done.1 = bf16[8,256,2]{0,2,1:T(2,128)(2,1)S(1)} async-done(((bf16[8,256,2]{0,2,1:T(2,128)(2,1)}), bf16[8,256,2]{0,2,1:T(2,128)(2,1)S(1)}, u32[]{:S(2)}, u32[]{:S(2)}) %all-to-all-start.1) | async-done | bytes 8224 | tf_op jit(solution)/shard_map/all_to_all | solution.py:53
  104.1 4.8 %all-to-all-start.3 = ((bf16[8,256,640]{2,0,1:T(8,128)(2,1)}), bf16[8,256,640]{2,0,1:T(8,128)(2,1)}, u32[]{:S(2)}, u32[]{:S(2)}) async-start(bf16[8,256,640]{2,0,1:T(8,128)(2,1)} %copy.55), calls=%async_computation.3 | async-start | bytes 5242880 | tf_op jit(solution)/shard_map/all_to_all | solution.py:52
  108.9 0.1 copy.52
  109.0 0.2 reshape.179
  109.2 0.2 copy.53
  109.3 0.2 reshape.178
  109.5 33.5 %all-to-all-done.3 = bf16[8,256,640]{2,0,1:T(8,128)(2,1)} async-done(((bf16[8,256,640]{2,0,1:T(8,128)(2,1)}), bf16[8,256,640]{2,0,1:T(8,128)(2,1)}, u32[]{:S(2)}, u32[]{:S(2)}) %all-to-all-start.3) | async-done | bytes 2621472 | tf_op jit(solution)/shard_map/all_to_all | solution.py:52
  143.0 0.0 copy-start.1
  143.0 0.0 copy-start.2
  143.0 0.0 copy-start.3
  143.0 2.4 copy.57
  145.4 0.0 copy-done.1
  145.4 0.1 copy-done.2
  145.5 0.4 copy-done.3
  145.9 4.5 %fusion.11 = (bf16[512,640]{1,0:T(8,128)(2,1)S(1)}, f32[512,640]{1,0:T(8,128)}, f32[512,640]{1,0:T(8,128)}, f32[512,640]{1,0:T(8,128)}) fusion(f32[512,640]{1,0:T(8,128)S(1)} %copy-done.1, f32[512,640]{1,0:T(8,128)S(1)} %copy-done.2, f32[512,640]{1,0:T(8,128)S(1)} %copy-done.3, bf16[2048,640]{1,0:T(8,128)(2,1)S(1)} %bitcast.49, f32[2048]{0:T(1024)S(1)} %bitcast.53), kind=kOutput, calls=%fused_computation.43 | convolution fusion | flops 1347813376 | bytes 11149312 | tf_op jit(solution)/shard_map/dot_general | solution.py:59
  150.3 0.4 stack.5
  150.7 120.6 %all_to_all.58 = bf16[8,512,640]{2,1,0:T(8,128)(2,1)} all-to-all(bf16[8,512,640]{2,1,0:T(8,128)(2,1)S(1)} %stack.5), channel_id=1, replica_groups=mesh['dp'=8,'vocab'=32] {'dp'}, dimensions={0} | all-to-all | bytes 10485760 | tf_op jit(solution)/shard_map/all_to_all | solution.py:18
  271.4 7.9 %copy.58 = bf16[8,512,640]{1,2,0:T(8,128)(2,1)} copy(bf16[8,512,640]{2,1,0:T(8,128)(2,1)} %all_to_all.58) | data formatting | bytes 10485760 | tf_op jit(solution)/shard_map/all_to_all | solution.py:18
  279.2 7.9 %copy.59 = bf16[512,5120]{1,0:T(8,128)(2,1)} copy(bf16[512,5120]{0,1:T(8,128)(2,1)} %bitcast.46) | data formatting | bytes 10485760
  (6 shorter events, 0.1 us)
Async XLA Ops:
  0.6 14.3 %copy-start = (bf16[256,5120]{1,0:T(8,128)(2,1)S(1)}, bf16[256,5120]{1,0:T(8,128)(2,1)}, u32[]{:S(2)}) copy-start(bf16[256,5120]{1,0:T(8,128)(2,1)} %param.8) | copy-start | bytes 7864324
  5.9 15.6 %all-to-all-start = ((bf16[256,8,2]{0,2,1:T(2,128)(2,1)}), bf16[256,8,2]{0,2,1:T(2,128)(2,1)S(1)}, u32[]{:S(2)}, u32[]{:S(2)}) async-start(bf16[256,8,2]{0,2,1:T(2,128)(2,1)} %tile.2), calls=%async_computation | async-start | bytes 16384 | tf_op jit(solution)/shard_map/all_to_all | solution.py:47
  21.5 64.0 %all-to-all-start.2 = ((bf16[256,8,640]{2,0,1:T(8,128)(2,1)}), bf16[256,8,640]{2,0,1:T(8,128)(2,1)}, u32[]{:S(2)}, u32[]{:S(2)}) async-start(bf16[256,8,640]{2,0,1:T(8,128)(2,1)} %bitcast.47), calls=%async_computation.2 | async-start | bytes 5242880 | tf_op jit(solution)/shard_map/all_to_all | solution.py:46
  85.5 18.6 %all-to-all-start.1 = ((bf16[8,256,2]{0,2,1:T(2,128)(2,1)}), bf16[8,256,2]{0,2,1:T(2,128)(2,1)S(1)}, u32[]{:S(2)}, u32[]{:S(2)}) async-start(bf16[8,256,2]{0,2,1:T(2,128)(2,1)} %copy.51), calls=%async_computation.1 | async-start | bytes 262144 | tf_op jit(solution)/shard_map/all_to_all | solution.py:53
  104.1 38.9 %all-to-all-start.3 = ((bf16[8,256,640]{2,0,1:T(8,128)(2,1)}), bf16[8,256,640]{2,0,1:T(8,128)(2,1)}, u32[]{:S(2)}, u32[]{:S(2)}) async-start(bf16[8,256,640]{2,0,1:T(8,128)(2,1)} %copy.55), calls=%async_computation.3 | async-start | bytes 5242880 | tf_op jit(solution)/shard_map/all_to_all | solution.py:52
  143.0 2.4 copy-start.1
  143.0 2.5 copy-start.2
  143.0 2.9 %copy-start.3 = (f32[512,640]{1,0:T(8,128)S(1)}, f32[512,640]{1,0:T(8,128)}, u32[]{:S(2)}) copy-start(f32[512,640]{1,0:T(8,128)} %param.11) | copy-start | bytes 3932164
